TPU v7x, 32 devices: a whole 2x2x4 slice. The times are simulated.
32 devices in a mesh: section: 4 (over y, x), mp: 8 (over z, core).
Axes of the slice: x: 2, y: 2, z: 4, core: 2. Of those that a mesh axis runs over, the one named last changes fastest.
Arguments:
- hidden_in: bfloat16 [1, 4, 64, 4096], P(None, 'section'), may hold values from -36 to 36
- attn_gain: bfloat16 [4, 4096], P('section'), may hold values from 0.5 to 2
- w_query: bfloat16 [4, 4096, 4096], P('section', None, 'mp'), may hold values from -0.75 to 0.75
- w_key: bfloat16 [4, 4096, 1024], P('section', None, 'mp'), may hold values from -0.0625 to 0.0625
- w_value: bfloat16 [4, 4096, 1024], P('section', None, 'mp'), may hold values from -0.09375 to 0.09375
- w_out: bfloat16 [4, 4096, 4096], P('section', 'mp'), may hold values from -0.09375 to 0.09375
- ffn_gain: bfloat16 [4, 4096], P('section'), may hold values from 0.5 to 2
- w_gate: bfloat16 [4, 4096, 14336], P('section', None, 'mp'), may hold values from -0.09375 to 0.09375
- w_up: bfloat16 [4, 4096, 14336], P('section', None, 'mp'), may hold values from -0.09375 to 0.09375
- w_down: bfloat16 [4, 14336, 4096], P('section', 'mp'), may hold values from -0.046875 to 0.046875
- ffn_blocks: int32 [4, 4], P(None, 'section'), may hold values from 1 to 112
- heads_on: int32 [4, 4], P(None, 'section'), may hold values from 1 to 32
Outputs:
- hidden_out: bfloat16 [1, 4, 64, 4096], P(None, 'section')
Inputs may be any that keep to these rules, and one draw needn't show every extreme that they name: `ffn_blocks`: hidden units below 128 times the entry are active. `heads_on`: query heads below the entry are active.
All inputs are finite; a program needn't handle non-finite values.
Results may differ from a plain program's by a relative error of at most 0.025.
Values may be sent and summed in bfloat16 or wider, within the bound.
A program may use at most 128 MiB of HBM per device.

v0:
```python
import jax
import jax.numpy as jnp
import numpy as np
from jax import lax
from jax.experimental import pallas as pl
from jax.experimental.pallas import tpu as pltpu
from jax.sharding import PartitionSpec as P

HEADS = 32
KV_HEADS = 8
HD = 128
BLOCK = 128


ROPE_BASE = 500000.0
EPSILON = 1e-05


def passed_along(array, axis, by):
    peers = lax.axis_size(axis)
    return lax.ppermute(array, axis, [(i, (i + by) % peers) for i in range(peers)])


def rms_scale(values, gain_row):
    mean_sq = jnp.mean(values * values, axis=-1, keepdims=True)
    return values * lax.rsqrt(mean_sq + EPSILON) * gain_row.astype(jnp.float32)


def rotate(values):
    length = values.shape[0]
    half_dim = values.shape[-1] // 2
    frequency = ROPE_BASE ** (-(jnp.arange(half_dim, dtype=jnp.float32) / half_dim))
    angles = jnp.arange(length, dtype=jnp.float32)[:, None] * frequency[None, :]
    cosine_table = jnp.cos(angles)[:, None, :]
    sine_table = jnp.sin(angles)[:, None, :]
    front_half = values[..., :half_dim].astype(jnp.float32)
    back_half = values[..., half_dim:].astype(jnp.float32)
    return jnp.concatenate(
        [
            front_half * cosine_table - back_half * sine_table,
            front_half * sine_table + back_half * cosine_table,
        ],
        axis=-1,
    )


def attend_local(projected, query_width, key_width, active, first_head):
    length = projected.shape[0]
    heads_here = query_width // HD
    group_size = HEADS // KV_HEADS
    queries = rotate(projected[:, :query_width].reshape(length, heads_here, HD)).astype(
        jnp.bfloat16
    )
    key_local = projected[:, query_width : query_width + key_width].astype(jnp.bfloat16)
    value_local = projected[:, query_width + key_width :].astype(jnp.bfloat16)
    key_whole, value_whole = (
        lax.all_gather(key_local, "mp", axis=1, tiled=True),
        lax.all_gather(value_local, "mp", axis=1, tiled=True),
    )
    key_heads = key_whole.reshape(length, HD, KV_HEADS).transpose(0, 2, 1)
    value_heads = value_whole.reshape(length, HD, KV_HEADS).transpose(0, 2, 1)
    kv_here = max(1, heads_here // group_size)
    repeat_count = heads_here // kv_here
    first_kv = first_head // group_size
    key_pick = lax.dynamic_slice_in_dim(key_heads, first_kv, kv_here, 1)
    value_pick = lax.dynamic_slice_in_dim(value_heads, first_kv, kv_here, 1)
    keys_rot = jnp.repeat(rotate(key_pick).astype(jnp.bfloat16), repeat_count, axis=1)
    values = jnp.repeat(value_pick, repeat_count, axis=1)
    scores = jnp.einsum(
        "qhd,khd->hqk", queries, keys_rot, preferred_element_type=jnp.float32
    ) * HD ** (-0.5)
    causal = jnp.arange(length)[:, None] >= jnp.arange(length)[None, :]
    scores = jnp.where(causal[None], scores, -jnp.inf)
    probabilities = jax.nn.softmax(scores, axis=-1).astype(jnp.bfloat16)
    context = jnp.einsum("hqk,khd->qhd", probabilities, values, preferred_element_type=jnp.float32)
    head_ids = first_head + jnp.arange(heads_here)
    context = jnp.where((head_ids < active)[None, :, None], context, 0.0).astype(jnp.bfloat16)
    return context.reshape(length, query_width)


def per_device(
    hidden_in,
    attn_gain,
    w_query,
    w_key,
    w_value,
    w_out,
    ffn_gain,
    w_gate,
    w_up,
    w_down,
    ffn_blocks,
    heads_on,
):
    section_count = lax.axis_size("section")
    section_index = lax.axis_index("section")
    model_count = lax.axis_size("mp")
    model_index = lax.axis_index("mp")
    micro_total = ffn_blocks.shape[0]
    per_section = hidden_in.shape[0]
    length = hidden_in.shape[2]
    model_width = hidden_in.shape[3]
    local_rows = length // model_count
    units_here = w_gate.shape[2]
    query_width = w_query.shape[2]
    key_width = w_key.shape[2]
    first_head = model_index * (query_width // HD)
    first_unit = model_index * units_here
    joined_qkv = [jnp.concatenate([w_query[0], w_key[0], w_value[0]], axis=1)]
    joined_pair = [jnp.concatenate([w_gate[0], w_up[0]], axis=1)]

    def gated(pre_act, block_count):
        gate_part = pre_act[:, :units_here]
        up_part = pre_act[:, units_here:]
        unit_ids = first_unit + jnp.arange(units_here)
        return jnp.where(
            (unit_ids < BLOCK * block_count)[None, :], jax.nn.silu(gate_part) * up_part, 0.0
        ).astype(jnp.bfloat16)

    def layer_rows(carried, layer_pos, active, block_count):
        residual = carried.astype(jnp.float32)
        normed = rms_scale(residual, attn_gain[layer_pos]).astype(jnp.bfloat16)
        projected = jnp.dot(
            lax.all_gather(normed, "mp", axis=0, tiled=True),
            joined_qkv[layer_pos],
            preferred_element_type=jnp.float32,
        )
        context = attend_local(projected, query_width, key_width, active, first_head)
        attended = residual + lax.psum_scatter(
            jnp.dot(context, w_out[layer_pos], preferred_element_type=jnp.float32).astype(
                jnp.bfloat16
            ),
            "mp",
            scatter_dimension=0,
            tiled=True,
        ).astype(jnp.float32)
        normed_ffn = rms_scale(attended, ffn_gain[layer_pos]).astype(jnp.bfloat16)
        hidden = gated(
            jnp.dot(
                lax.all_gather(normed_ffn, "mp", axis=0, tiled=True),
                joined_pair[layer_pos],
                preferred_element_type=jnp.float32,
            ),
            block_count,
        )
        return (
            attended
            + lax.psum_scatter(
                jnp.dot(hidden, w_down[layer_pos], preferred_element_type=jnp.float32).astype(
                    jnp.bfloat16
                ),
                "mp",
                scatter_dimension=0,
                tiled=True,
            ).astype(jnp.float32)
        ).astype(jnp.bfloat16)

    def section_work(carried, moment, layer_fn):
        micro_index = jnp.clip(moment - section_index, 0, micro_total - 1)
        carried = layer_fn(carried, 0, heads_on[micro_index, 0], ffn_blocks[micro_index, 0])
        return carried

    def tick_step(moment, loop_carry):
        carried, slot_buffer = loop_carry
        cycle_index = moment // section_count
        incoming = lax.dynamic_index_in_dim(
            slot_buffer, jnp.minimum(cycle_index, per_section - 1), 0, keepdims=False
        )
        incoming = jnp.where(moment < micro_total, incoming, jnp.zeros_like(incoming))
        at_head = section_index == 0
        written = lax.dynamic_update_index_in_dim(
            slot_buffer, carried, jnp.maximum(cycle_index - 1, 0), 0
        )
        slot_buffer = jnp.where(at_head & (moment >= section_count), written, slot_buffer)
        carried = jnp.where(at_head, incoming, carried)
        carried = section_work(carried, moment, layer_rows)
        carried = passed_along(carried, "section", 1)
        slot_buffer = passed_along(slot_buffer, "section", -1)
        return (carried, slot_buffer)

    slot_start = hidden_in.reshape(per_section, length, model_width)
    slot_start = lax.dynamic_slice_in_dim(slot_start, model_index * local_rows, local_rows, 1)
    initial = jnp.zeros((local_rows, model_width), jnp.bfloat16)
    finished = lax.fori_loop(0, micro_total + section_count, tick_step, (initial, slot_start))
    result = finished[1]
    result = lax.all_gather(result, "mp", axis=1, tiled=True)
    return result.reshape(hidden_in.shape)


MESH = pl.DeviceIdType.MESH
BF16 = jnp.bfloat16
F32 = jnp.float32
TILE = 256
WIDE = 512


def tables(length):
    half = HD // 2
    frequency = np.float32(ROPE_BASE) ** (-(np.arange(half, dtype=np.float32) / np.float32(half)))
    angles = np.arange(length, dtype=np.float32)[:, None] * frequency[None, :].astype(np.float32)
    cosine, sine = np.cos(angles), np.sin(angles)
    q_cos = np.concatenate([cosine, cosine], axis=1)
    q_sin = np.concatenate([-sine, sine], axis=1)
    k_cos = np.concatenate([q_cos.T, np.ones((HD, length))], axis=1)
    k_sin = np.concatenate([q_sin.T, np.zeros((HD, length))], axis=1)
    return [jnp.asarray(t, F32) for t in (q_cos, q_sin, k_cos, k_sin)]


def remote(src, dst, send_sem, recv_sem, where):
    return pltpu.make_async_remote_copy(
        src_ref=src,
        dst_ref=dst,
        send_sem=send_sem,
        recv_sem=recv_sem,
        device_id=where,
        device_id_type=MESH,
    )


def layer_kernel(
    sections,
    peers,
    heads_on,
    ffn_blocks,
    hidden_in,
    attn_gain,
    ffn_gain,
    q_cos,
    q_sin,
    k_cos,
    k_sin,
    w_query,
    w_key,
    w_value,
    w_out,
    w_gate,
    w_up,
    w_down,
    out,
    v_query,
    v_kv,
    v_out,
    v_gate,
    v_up,
    v_down,
    inbox,
    outbox,
    home,
    rows_f32,
    gathered,
    normed,
    kv_send,
    kv_recv,
    context,
    hidden,
    part,
    pair_in,
    chip_send,
    chip_in,
    weight_sem,
    inbox_sem,
    outbox_sem,
    seed_sem,
    home_sem,
    gather_send,
    gather_recv,
    relay_send,
    relay_recv,
    kv_send_sem,
    kv_recv_sem,
    pair_sem,
    chip_send_sem,
    chip_recv_sem,
    out_sem,
):
    sec = lax.axis_index("section")
    me = lax.axis_index("mp")
    chips = peers // 2
    chip, core = me // 2, me % 2
    slot = core * chips + chip
    mate = (sec, chip * 2 + 1 - core)
    last = sections - 1
    rows, width = rows_f32.shape
    length = peers * rows
    heads_here = v_query.shape[1] // HD
    key_width = w_key.shape[1]
    units = v_gate.shape[1]

    def chip_at(step):
        other = (chip + step) % chips
        return other, (sec, other * 2 + core)

    def weight_copies():
        pairs = (
            (w_query, v_query),
            (w_key, v_kv.at[:, pl.ds(0, key_width)]),
            (w_value, v_kv.at[:, pl.ds(key_width, key_width)]),
            (w_out, v_out),
            (w_gate, v_gate),
            (w_up, v_up),
            (w_down, v_down),
        )
        return [
            pltpu.make_async_copy(a, b, weight_sem.at[i]) for i, (a, b) in enumerate(pairs)
        ]

    seed = pltpu.make_async_copy(hidden_in.at[slot], home, seed_sem)
    seed.start()
    for copy in weight_copies():
        copy.start()

    barrier = pltpu.get_barrier_semaphore()
    for step in range(1, peers):
        pl.semaphore_signal(barrier, inc=1, device_id=(sec, (me + step) % peers), device_id_type=MESH)
    for step in range(1, sections):
        pl.semaphore_signal(barrier, inc=1, device_id=((sec + step) % sections, me), device_id_type=MESH)
    pl.semaphore_wait(barrier, peers + sections - 2)

    seed.wait()
    own = remote(home, inbox.at[sec], outbox_sem.at[0], inbox_sem.at[sec], (0, me))

    @pl.when(sec == 0)
    def _():
        inbox[0] = home[...]

    @pl.when(sec != 0)
    def _():
        own.start()
        own.wait_send()

    def all_gather():
        mine = gathered.at[slot]
        to_mate = remote(mine, mine, gather_send.at[chips - 1], gather_recv.at[chips - 1], mate)
        sends = []
        for k in (list(range(1, chips, 2)) + list(range(2, chips, 2))):
            _, where = chip_at(k)
            sends.append(remote(mine, mine, gather_send.at[k - 1], gather_recv.at[k - 1], where))
            sends[-1].start()
        to_mate.start()
        relays = []
        for k in (list(range(1, chips, 2)) + list(range(2, chips, 2))):
            other, where = chip_at(chips - k)
            block = gathered.at[core * chips + other]
            remote(block, block, gather_send.at[k - 1], gather_recv.at[k - 1], where).wait_recv()
            relays.append(remote(block, block, relay_send.at[k - 1], relay_recv.at[k - 1], mate))
            relays[-1].start()
        to_mate.wait_recv()
        for k in range(1, chips):
            other, _ = chip_at(chips - k)
            block = gathered.at[(1 - core) * chips + other]
            remote(block, block, relay_send.at[k - 1], relay_recv.at[k - 1], mate).wait_recv()
        for copy in sends + relays + [to_mate]:
            copy.wait_send()

    def widen():
        columns = width // 4
        for i in range(4):
            at = pl.ds(i * columns, columns)
            block = gathered[:, :, at].astype(F32)
            normed[:, at] = block.reshape(length, columns).astype(BF16)

    def norm_rows(gain):
        x = rows_f32[...]
        scale = lax.rsqrt(jnp.mean(x * x, axis=-1, keepdims=True) + EPSILON)
        gathered[slot] = (x * scale * gain[...].astype(F32)).astype(BF16)

    def reduce_rows():
        other_half = part.at[pl.ds((1 - core) * chips, chips)]
        across = remote(other_half, pair_in, pair_sem.at[0], pair_sem.at[1], mate)
        across.start()
        across.wait_recv()
        for k in range(1, chips):
            other, where = chip_at(k)
            both = part[core * chips + other].astype(F32) + pair_in[other].astype(F32)
            chip_send[k - 1] = both.astype(BF16)
            remote(
                chip_send.at[k - 1], chip_in.at[k - 1], chip_send_sem.at[k - 1], chip_recv_sem.at[k - 1], where
            ).start()
        rows_f32[...] = rows_f32[...] + (part[slot].astype(F32) + pair_in[chip].astype(F32))
        for k in range(1, chips):
            _, where = chip_at(k)
            remote(
                chip_send.at[k - 1], chip_in.at[k - 1], chip_send_sem.at[k - 1], chip_recv_sem.at[k - 1], where
            ).wait()
            rows_f32[...] = rows_f32[...] + chip_in[k - 1].astype(F32)
        across.wait_send()

    def project_rows(left, weight):
        def step(i, _):
            at = pl.ds(pl.multiple_of(i * WIDE, WIDE), WIDE)
            term = jnp.dot(left[...], weight[:, at], preferred_element_type=F32)
            part[:, :, at] = term.reshape(peers, rows, WIDE).astype(BF16)
            return 0

        lax.fori_loop(0, width // WIDE, step, 0)

    def exchange_kv():
        copies = []
        for step in range(1, peers):
            to = (me + step) % peers
            copies.append(
                remote(
                    kv_send.at[to], kv_recv.at[me], kv_send_sem.at[step - 1], kv_recv_sem.at[step - 1], (sec, to)
                )
            )
            copies[-1].start()
        kv_recv[me] = kv_send[me]
        return copies

    def attention(active):
        left = normed[...]
        kv = jnp.dot(left, v_kv[...], preferred_element_type=F32).astype(BF16)
        stacked = jnp.concatenate([kv[:, :key_width], kv[:, key_width:]], axis=0)
        r = lax.broadcasted_iota(jnp.int32, (key_width, key_width), 0)
        c = lax.broadcasted_iota(jnp.int32, (key_width, key_width), 1)
        parts_here = key_width // KV_HEADS
        pick = jnp.where(c == (r % parts_here) * KV_HEADS + r // parts_here, 1.0, 0.0).astype(BF16)
        by_head = lax.dot_general(
            pick, stacked, (((1,), (1,)), ((), ())), preferred_element_type=F32
        )
        kv_send[...] = by_head.astype(BF16).reshape(KV_HEADS, parts_here, 2 * length)
        copies = exchange_kv()
        query = jnp.dot(left, v_query[...], preferred_element_type=F32)
        heads = []
        for h in range(heads_here):
            head = query[:, h * HD : (h + 1) * HD]
            heads.append(
                (head * q_cos[...] + pltpu.roll(head, HD // 2, 1) * q_sin[...]).astype(BF16)
            )
        queries = jnp.concatenate(heads, axis=0)
        for copy in copies:
            copy.wait()
        pair = kv_recv[...].reshape(HD, 2 * length).astype(F32)
        swapped = jnp.concatenate([pair[HD // 2 :], pair[: HD // 2]], axis=0)
        pair = (pair * k_cos[...] + swapped * k_sin[...]).astype(BF16)
        scores = jnp.dot(queries, pair, preferred_element_type=F32) * HD ** (-0.5)
        token = lax.broadcasted_iota(jnp.int32, scores.shape, 0) % length
        key_at = lax.broadcasted_iota(jnp.int32, scores.shape, 1)
        scores = jnp.where(key_at <= token, scores, -jnp.inf)
        scores = jnp.exp(scores - jnp.max(scores, axis=-1, keepdims=True))
        chances = scores / jnp.sum(scores, axis=-1, keepdims=True)
        chances = pltpu.roll(chances, length, 1).astype(BF16)
        mixed = lax.dot_general(
            chances, pair, (((1,), (1,)), ((), ())), preferred_element_type=F32
        )
        for h in range(heads_here):
            on = me * heads_here + h < active
            block = mixed[h * length : (h + 1) * length]
            context[:, h * HD : (h + 1) * HD] = jnp.where(on, block, 0.0).astype(BF16)

    def feed_forward(block_count):
        def step(i, _):
            at = pl.ds(pl.multiple_of(i * TILE, TILE), TILE)
            left = normed[...]
            gate = jnp.dot(left, v_gate[:, at], preferred_element_type=F32)
            up = jnp.dot(left, v_up[:, at], preferred_element_type=F32)
            unit = me * units + i * TILE + lax.broadcasted_iota(jnp.int32, gate.shape, 1)
            value = gate / (1.0 + jnp.exp(-gate)) * up
            hidden[:, at] = jnp.where(unit < BLOCK * block_count, value, 0.0).astype(BF16)
            return 0

        lax.fori_loop(0, units // TILE, step, 0)

    def micro_step(m, _):
        arrived = remote(home, inbox.at[m], outbox_sem.at[0], inbox_sem.at[m], (0, me))

        @pl.when((sec != 0) | (m != 0))
        def _():
            arrived.wait_recv()

        rows_f32[...] = inbox[m].astype(F32)
        norm_rows(attn_gain)
        all_gather()
        widen()

        def when_loaded(first, stop):
            @pl.when(m == 0)
            def _():
                for copy in weight_copies()[first:stop]:
                    copy.wait()

        when_loaded(0, 3)
        attention(heads_on[m, 0])
        when_loaded(3, 4)
        project_rows(context, v_out)
        reduce_rows()
        norm_rows(ffn_gain)
        all_gather()
        widen()
        when_loaded(4, 6)
        feed_forward(ffn_blocks[m, 0])
        when_loaded(6, 7)
        project_rows(hidden, v_down)
        reduce_rows()
        outbox[m] = rows_f32[...].astype(BF16)

        @pl.when(sec < last)
        def _():
            remote(outbox.at[m], inbox.at[m], outbox_sem.at[m], inbox_sem.at[m], (sec + 1, me)).start()

        @pl.when((sec == last) & (m < last))
        def _():
            remote(outbox.at[m], home, outbox_sem.at[m], home_sem, (m, me)).start()

        return 0

    lax.fori_loop(0, sections, micro_step, 0)

    for m in range(sections):
        sent = remote(outbox.at[m], home, outbox_sem.at[m], home_sem, (0, me))
        if m < last:
            sent.wait_send()
        else:

            @pl.when(sec < last)
            def _():
                sent.wait_send()

    @pl.when(sec < last)
    def _():
        remote(outbox.at[0], home, outbox_sem.at[0], home_sem, (last, me)).wait_recv()
        gathered[slot] = home[...]

    @pl.when(sec == last)
    def _():
        gathered[slot] = outbox[last]

    all_gather()
    done = pltpu.make_async_copy(gathered, out, out_sem)
    done.start()
    done.wait()


def resident(hidden_in, attn_gain, w_query, w_key, w_value, w_out, ffn_gain, w_gate, w_up, w_down, ffn_blocks, heads_on):
    sections, peers = lax.axis_size("section"), lax.axis_size("mp")
    length, width = hidden_in.shape[2:]
    rows, chips = length // peers, peers // 2
    units, key_width = w_gate.shape[2], w_key.shape[2]
    query_width = w_query.shape[2]
    parts_here = key_width // KV_HEADS
    smem = pl.BlockSpec(memory_space=pltpu.SMEM)
    vmem = pl.BlockSpec(memory_space=pltpu.VMEM)
    hbm = pl.BlockSpec(memory_space=pl.ANY)
    dma = pltpu.SemaphoreType.DMA
    half = pltpu.VMEM
    result = pl.pallas_call(
        lambda *refs: layer_kernel(sections, peers, *refs),
        out_shape=jax.ShapeDtypeStruct((peers, rows, width), BF16),
        in_specs=[smem, smem, hbm] + [vmem] * 6 + [hbm] * 7,
        out_specs=hbm,
        scratch_shapes=[
            half((width, query_width), BF16),
            half((width, 2 * key_width), BF16),
            half((query_width, width), BF16),
            half((width, units), BF16),
            half((width, units), BF16),
            half((units, width), BF16),
            half((sections, rows, width), BF16),
            half((sections, rows, width), BF16),
            half((rows, width), BF16),
            half((rows, width), F32),
            half((peers, rows, width), BF16),
            half((length, width), BF16),
            half((peers, parts_here, 2 * length), BF16),
            half((peers, parts_here, 2 * length), BF16),
            half((length, query_width), BF16),
            half((length, units), BF16),
            half((peers, rows, width), BF16),
            half((chips, rows, width), BF16),
            half((chips - 1, rows, width), BF16),
            half((chips - 1, rows, width), BF16),
            dma((7,)),
            dma((sections,)),
            dma((sections,)),
            dma,
            dma,
            dma((chips,)),
            dma((chips,)),
            dma((chips - 1,)),
            dma((chips - 1,)),
            dma((peers - 1,)),
            dma((peers - 1,)),
            dma((2,)),
            dma((chips - 1,)),
            dma((chips - 1,)),
            dma,
        ],
        compiler_params=pltpu.CompilerParams(
            collective_id=0, has_side_effects=True, vmem_limit_bytes=67043328
        ),
    )(
        heads_on,
        ffn_blocks,
        hidden_in.reshape(peers, rows, width),
        attn_gain,
        ffn_gain,
        *tables(length),
        w_query[0],
        w_key[0],
        w_value[0],
        w_out[0],
        w_gate[0],
        w_up[0],
        w_down[0],
    )
    return result.reshape(hidden_in.shape)


def one_device(*args):
    hidden_in, w_query, w_key, w_gate = args[0], args[2], args[3], args[7]
    sections, peers = lax.axis_size("section"), lax.axis_size("mp")
    fits = (
        hidden_in.shape[0] == 1
        and args[10].shape[0] == sections
        and peers == KV_HEADS
        and hidden_in.shape[2] == 8 * peers
        and 2 * hidden_in.shape[2] == HD
        and w_query.shape[2] * KV_HEADS == HEADS * HD
        and w_key.shape[2] == HD
        and w_gate.shape[2] % TILE == 0
        and hidden_in.shape[3] % WIDE == 0
    )
    return (resident if fits else per_device)(*args)


def solution(mesh):
    return jax.shard_map(
        one_device,
        mesh=mesh,
        in_specs=(
            P(None, "section", None, None),
            P("section", None),
            P("section", None, "mp"),
            P("section", None, "mp"),
            P("section", None, "mp"),
            P("section", "mp", None),
            P("section", None),
            P("section", None, "mp"),
            P("section", None, "mp"),
            P("section", "mp", None),
            P(None, "section"),
            P(None, "section"),
        ),
        out_specs=P(None, "section", None, None),
        check_vma=False,
    )
```

profile of v0, /device:TPU:7, one launch (start us, length us, event | category | flops | bytes accessed | tf_op | source)
XLA Modules:
  0.0 390.5 jit_solution(13336235050429360747)
XLA Ops:
  0.0 1.3 copy.18.refs_1_
  1.3 1.3 copy.17.refs_0_
  2.6 386.0 %shard_map.154 = bf16[8,8,4096]{2,1,0:T(8,128)(2,1)} custom-call(s32[4,1]{1,0:T(4,128)} %copy.17.refs_0_, s32[4,1]{1,0:T(4,128)} %copy.18.refs_1_, bf16[8,8,4096]{2,1,0:T(8,128)(2,1)} %bitcast.17, bf16[1,4096]{1,0:T(2,128)(2,1)} %refs_3_.1, bf16[1,4096]{1,0:T(2,128)(2,1)} %refs_4_.1, f32[64,128]{1,0:T(8,128)} %constant.8.clone.refs_5_, ...), custom_call_target="tpu_custom_call" | custom-call | tf_op jit(solution)/shard_map/pallas_call | solution.py:546
  388.7 1.9 copy.20
where the time goes:
time: 391 us
  Pallas kernels  386 us (99%)
  local copies, waits for them, and re-layouts  4.51 us (1%)
    pallas_call x1, Pallas kernels, resident(): pl.pallas_call(lambda *refs: layer_kernel(sections, peers, *refs), out_sh...  386 us

commit v1 on v0

--- a/solution.py
+++ b/solution.py
@@ -191,7 +191,6 @@
 BF16 = jnp.bfloat16
 F32 = jnp.float32
 TILE = 256
-WIDE = 512
 
 
 def tables(length):
@@ -220,8 +219,8 @@
 def layer_kernel(
     sections,
     peers,
-    heads_on,
-    ffn_blocks,
+    heads_hbm,
+    blocks_hbm,
     hidden_in,
     attn_gain,
     ffn_gain,
@@ -243,58 +242,83 @@
     v_gate,
     v_up,
     v_down,
-    inbox,
-    outbox,
-    home,
-    rows_f32,
-    gathered,
-    normed,
+    heads_on,
+    ffn_blocks,
+    gains,
+    x_in,
+    x_ffn,
+    final,
+    scaled,
+    squares,
+    residual,
+    query_buf,
     kv_send,
     kv_recv,
     context,
+    acc_gate,
+    acc_up,
     hidden,
-    part,
+    pair_send,
     pair_in,
     chip_send,
     chip_in,
+    result,
     weight_sem,
-    inbox_sem,
-    outbox_sem,
-    seed_sem,
-    home_sem,
-    gather_send,
-    gather_recv,
-    relay_send,
-    relay_recv,
+    small_sem,
+    stage_sem,
+    seed_send,
+    seed_recv,
+    x_recv,
+    x_relay_send,
+    x_relay_recv,
     kv_send_sem,
     kv_recv_sem,
-    pair_sem,
+    pair_send_sem,
+    pair_recv_sem,
     chip_send_sem,
     chip_recv_sem,
+    ffn_mate_send,
+    ffn_mate_recv,
+    ffn_send,
+    ffn_recv,
+    ffn_relay_send,
+    ffn_relay_recv,
+    result_send,
+    final_recv,
+    final_relay_send,
+    final_relay_recv,
     out_sem,
 ):
     sec = lax.axis_index("section")
     me = lax.axis_index("mp")
     chips = peers // 2
     chip, core = me // 2, me % 2
-    slot = core * chips + chip
-    mate = (sec, chip * 2 + 1 - core)
+    mate_at = chip * 2 + 1 - core
+    mate = (sec, mate_at)
     last = sections - 1
-    rows, width = rows_f32.shape
-    length = peers * rows
+    length, block = x_in.shape[2:]
+    width = peers * block
     heads_here = v_query.shape[1] // HD
     key_width = w_key.shape[1]
     units = v_gate.shape[1]
-
-    def chip_at(step):
-        other = (chip + step) % chips
-        return other, (sec, other * 2 + core)
+    high = chip // 2
+    near = (chip, chip + 1 - 2 * (chip % 2), 2 - high, 3 * (1 - high))
+    far = near[::-1]
+
+    def nth(order, i):
+        value = order[0]
+        for k in range(1, len(order)):
+            value = jnp.where(i == k, order[k], value)
+        return value
+
+    def offset(source, target):
+        return (source - target + chips) % chips - 1
 
     def weight_copies():
         pairs = (
-            (w_query, v_query),
             (w_key, v_kv.at[:, pl.ds(0, key_width)]),
             (w_value, v_kv.at[:, pl.ds(key_width, key_width)]),
+            (w_query, v_query),
             (w_out, v_out),
             (w_gate, v_gate),
             (w_up, v_up),
@@ -304,8 +328,32 @@
             pltpu.make_async_copy(a, b, weight_sem.at[i]) for i, (a, b) in enumerate(pairs)
         ]
 
-    seed = pltpu.make_async_copy(hidden_in.at[slot], home, seed_sem)
-    seed.start()
+    def columns(j):
+        return pl.ds(pl.multiple_of(j * block, block), block)
+
+    small = [
+        pltpu.make_async_copy(heads_hbm, heads_on, small_sem.at[0]),
+        pltpu.make_async_copy(blocks_hbm, ffn_blocks, small_sem.at[1]),
+    ]
+    for copy in small:
+        copy.start()
+
+    def staged(target):
+        return [
+            pltpu.make_async_copy(hidden_in.at[:, pl.ds(j * block, block)], target.at[j], stage_sem.at[j])
+            for j in range(peers)
+        ]
+
+    @pl.when(sec == 0)
+    def _():
+        for copy in staged(x_in.at[0]):
+            copy.start()
+
+    @pl.when(sec != 0)
+    def _():
+        for copy in staged(final):
+            copy.start()
+
     for copy in weight_copies():
         copy.start()
 
@@ -313,103 +361,155 @@
     for step in range(1, peers):
         pl.semaphore_signal(barrier, inc=1, device_id=(sec, (me + step) % peers), device_id_type=MESH)
     for step in range(1, sections):
-        pl.semaphore_signal(barrier, inc=1, device_id=((sec + step) % sections, me), device_id_type=MESH)
-    pl.semaphore_wait(barrier, peers + sections - 2)
-
-    seed.wait()
-    own = remote(home, inbox.at[sec], outbox_sem.at[0], inbox_sem.at[sec], (0, me))
+        for away in range(chips):
+            pl.semaphore_signal(
+                barrier,
+                inc=1,
+                device_id=((sec + step) % sections, (chip + away) % chips * 2 + core),
+                device_id_type=MESH,
+            )
+    pl.semaphore_wait(barrier, peers - 1 + (sections - 1) * chips)
+
+    seed = remote(final, x_in.at[sec], seed_send, seed_recv.at[sec], (0, me))
 
     @pl.when(sec == 0)
     def _():
-        inbox[0] = home[...]
+        for copy in staged(x_in.at[0]):
+            copy.wait()
 
     @pl.when(sec != 0)
     def _():
-        own.start()
-        own.wait_send()
-
-    def all_gather():
-        mine = gathered.at[slot]
-        to_mate = remote(mine, mine, gather_send.at[chips - 1], gather_recv.at[chips - 1], mate)
-        sends = []
-        for k in (list(range(1, chips, 2)) + list(range(2, chips, 2))):
-            _, where = chip_at(k)
-            sends.append(remote(mine, mine, gather_send.at[k - 1], gather_recv.at[k - 1], where))
-            sends[-1].start()
-        to_mate.start()
-        relays = []
-        for k in (list(range(1, chips, 2)) + list(range(2, chips, 2))):
-            other, where = chip_at(chips - k)
-            block = gathered.at[core * chips + other]
-            remote(block, block, gather_send.at[k - 1], gather_recv.at[k - 1], where).wait_recv()
-            relays.append(remote(block, block, relay_send.at[k - 1], relay_recv.at[k - 1], mate))
-            relays[-1].start()
-        to_mate.wait_recv()
-        for k in range(1, chips):
-            other, _ = chip_at(chips - k)
-            block = gathered.at[(1 - core) * chips + other]
-            remote(block, block, relay_send.at[k - 1], relay_recv.at[k - 1], mate).wait_recv()
-        for copy in sends + relays + [to_mate]:
-            copy.wait_send()
-
-    def widen():
-        columns = width // 4
-        for i in range(4):
-            at = pl.ds(i * columns, columns)
-            block = gathered[:, :, at].astype(F32)
-            normed[:, at] = block.reshape(length, columns).astype(BF16)
-
-    def norm_rows(gain):
-        x = rows_f32[...]
-        scale = lax.rsqrt(jnp.mean(x * x, axis=-1, keepdims=True) + EPSILON)
-        gathered[slot] = (x * scale * gain[...].astype(F32)).astype(BF16)
-
-    def reduce_rows():
-        other_half = part.at[pl.ds((1 - core) * chips, chips)]
-        across = remote(other_half, pair_in, pair_sem.at[0], pair_sem.at[1], mate)
-        across.start()
-        across.wait_recv()
-        for k in range(1, chips):
-            other, where = chip_at(k)
-            both = part[core * chips + other].astype(F32) + pair_in[other].astype(F32)
-            chip_send[k - 1] = both.astype(BF16)
-            remote(
-                chip_send.at[k - 1], chip_in.at[k - 1], chip_send_sem.at[k - 1], chip_recv_sem.at[k - 1], where
-            ).start()
-        rows_f32[...] = rows_f32[...] + (part[slot].astype(F32) + pair_in[chip].astype(F32))
-        for k in range(1, chips):
-            _, where = chip_at(k)
-            remote(
-                chip_send.at[k - 1], chip_in.at[k - 1], chip_send_sem.at[k - 1], chip_recv_sem.at[k - 1], where
-            ).wait()
-            rows_f32[...] = rows_f32[...] + chip_in[k - 1].astype(F32)
-        across.wait_send()
-
-    def project_rows(left, weight):
-        def step(i, _):
-            at = pl.ds(pl.multiple_of(i * WIDE, WIDE), WIDE)
-            term = jnp.dot(left[...], weight[:, at], preferred_element_type=F32)
-            part[:, :, at] = term.reshape(peers, rows, WIDE).astype(BF16)
+        for copy in staged(final):
+            copy.wait()
+        seed.start()
+
+    for row, gain in enumerate((attn_gain, ffn_gain)):
+        for j in range(peers):
+            gains[row, j] = jnp.broadcast_to(
+                gain[:, j * block : (j + 1) * block].astype(F32), gains.shape[2:]
+            )
+    for copy in small:
+        copy.wait()
+
+    @pl.when(sec != 0)
+    def _():
+        seed.wait_send()
+
+    def row_scale():
+        total = jnp.sum(squares[...], axis=-1, keepdims=True)
+        return lax.rsqrt(total * (1.0 / width) + EPSILON)
+
+    def with_gain(row, j, values):
+        x = values.astype(F32)
+        part = x * x
+        total = part[:, :HD]
+        for k in range(1, block // HD):
+            total = total + part[:, k * HD : (k + 1) * HD]
+        squares[...] = squares[...] + total
+        return (x * gains[row, j, 0:1, :]).astype(BF16)
+
+    def x_direct(m, o, where):
+        j = o * 2 + core
+        return remote(x_in.at[m, j], x_in.at[m, j], result_send.at[m, o], x_recv.at[m, o], where)
+
+    def x_relay(m, o):
+        j = o * 2 + core
+        return remote(x_in.at[m, j], x_in.at[m, j], x_relay_send.at[m, o], x_relay_recv.at[m, o], mate)
+
+    def x_relayed(m, o):
+        j = o * 2 + 1 - core
+        return remote(x_in.at[m, j], x_in.at[m, j], x_relay_send.at[m, o], x_relay_recv.at[m, o], mate)
+
+    def kv_copy(slot, step):
+        to = (me + step) % peers
+        return remote(
+            kv_send.at[slot, to],
+            kv_recv.at[slot, me],
+            kv_send_sem.at[slot, step - 1],
+            kv_recv_sem.at[slot, step - 1],
+            (sec, to),
+        )
+
+    def pair_copy(slot, k):
+        return remote(
+            pair_send.at[slot, k], pair_in.at[slot, k], pair_send_sem.at[slot, k], pair_recv_sem.at[slot, k], mate
+        )
+
+    def chip_copy(slot, target):
+        i = offset(chip, target)
+        return remote(
+            chip_send.at[slot, i],
+            chip_in.at[slot, i],
+            chip_send_sem.at[slot, i],
+            chip_recv_sem.at[slot, i],
+            (sec, target * 2 + core),
+        )
+
+    def ffn_mate(slot):
+        return remote(
+            x_ffn.at[slot, me], x_ffn.at[slot, me], ffn_mate_send.at[slot], ffn_mate_recv.at[slot], mate
+        )
+
+    def ffn_direct(slot, target):
+        i = offset(chip, target)
+        return remote(
+            x_ffn.at[slot, me],
+            x_ffn.at[slot, me],
+            ffn_send.at[slot, i],
+            ffn_recv.at[slot, i],
+            (sec, target * 2 + core),
+        )
+
+    def ffn_arrival(slot, o):
+        j = o * 2 + core
+        i = offset(o, chip)
+        return remote(x_ffn.at[slot, j], x_ffn.at[slot, j], ffn_send.at[slot, i], ffn_recv.at[slot, i], mate)
+
+    def ffn_relay(slot, o, by):
+        j = o * 2 + by
+        i = offset(o, chip)
+        return remote(
+            x_ffn.at[slot, j], x_ffn.at[slot, j], ffn_relay_send.at[slot, i], ffn_relay_recv.at[slot, i], mate
+        )
+
+    def project(m):
+        slot = m % 2
+        squares[...] = jnp.zeros_like(squares)
+
+        @pl.when((sec == 0) & (m != 0))
+        def _():
+            remote(x_in.at[m], x_in.at[m], seed_send, seed_recv.at[m], mate).wait_recv()
+
+        def direct(i, _):
+            o = nth(near, i)
+
+            @pl.when(sec != 0)
+            def _():
+                x_direct(m, o, mate).wait_recv()
+                x_relay(m, o).start()
+
+            j = o * 2 + core
+            scaled[:, columns(j)] = with_gain(0, j, x_in[m, j])
             return 0
 
-        lax.fori_loop(0, width // WIDE, step, 0)
-
-    def exchange_kv():
-        copies = []
-        for step in range(1, peers):
-            to = (me + step) % peers
-            copies.append(
-                remote(
-                    kv_send.at[to], kv_recv.at[me], kv_send_sem.at[step - 1], kv_recv_sem.at[step - 1], (sec, to)
-                )
-            )
-            copies[-1].start()
-        kv_recv[me] = kv_send[me]
-        return copies
-
-    def attention(active):
-        left = normed[...]
-        kv = jnp.dot(left, v_kv[...], preferred_element_type=F32).astype(BF16)
+        lax.fori_loop(0, chips, direct, 0)
+
+        def relayed(i, _):
+            o = nth(near, i)
+
+            @pl.when(sec != 0)
+            def _():
+                x_relayed(m, o).wait_recv()
+
+            j = o * 2 + 1 - core
+            scaled[:, columns(j)] = with_gain(0, j, x_in[m, j])
+            return 0
+
+        lax.fori_loop(0, chips, relayed, 0)
+        when_loaded(m, 0, 3)
+        scale = row_scale()
+        left = scaled[...]
+        kv = (jnp.dot(left, v_kv[...], preferred_element_type=F32) * scale).astype(BF16)
         stacked = jnp.concatenate([kv[:, :key_width], kv[:, key_width:]], axis=0)
         r = lax.broadcasted_iota(jnp.int32, (key_width, key_width), 0)
         c = lax.broadcasted_iota(jnp.int32, (key_width, key_width), 1)
@@ -418,22 +518,25 @@
         by_head = lax.dot_general(
             pick, stacked, (((1,), (1,)), ((), ())), preferred_element_type=F32
         )
-        kv_send[...] = by_head.astype(BF16).reshape(KV_HEADS, parts_here, 2 * length)
-        copies = exchange_kv()
-        query = jnp.dot(left, v_query[...], preferred_element_type=F32)
-        heads = []
+        kv_send[slot] = by_head.astype(BF16).reshape(KV_HEADS, parts_here, 2 * length)
+        for step in range(1, peers):
+            kv_copy(slot, step).start()
+        kv_recv[slot, me] = kv_send[slot, me]
+        query = jnp.dot(left, v_query[...], preferred_element_type=F32) * scale
         for h in range(heads_here):
             head = query[:, h * HD : (h + 1) * HD]
-            heads.append(
-                (head * q_cos[...] + pltpu.roll(head, HD // 2, 1) * q_sin[...]).astype(BF16)
-            )
-        queries = jnp.concatenate(heads, axis=0)
-        for copy in copies:
-            copy.wait()
-        pair = kv_recv[...].reshape(HD, 2 * length).astype(F32)
+            query_buf[slot, pl.ds(h * length, length), :] = (
+                head * q_cos[...] + pltpu.roll(head, HD // 2, 1) * q_sin[...]
+            ).astype(BF16)
+
+    def attend(m):
+        slot = m % 2
+        for step in range(1, peers):
+            kv_copy(slot, step).wait()
+        pair = kv_recv[slot].reshape(HD, 2 * length).astype(F32)
         swapped = jnp.concatenate([pair[HD // 2 :], pair[: HD // 2]], axis=0)
         pair = (pair * k_cos[...] + swapped * k_sin[...]).astype(BF16)
-        scores = jnp.dot(queries, pair, preferred_element_type=F32) * HD ** (-0.5)
+        scores = jnp.dot(query_buf[slot], pair, preferred_element_type=F32) * HD ** (-0.5)
         token = lax.broadcasted_iota(jnp.int32, scores.shape, 0) % length
         key_at = lax.broadcasted_iota(jnp.int32, scores.shape, 1)
         scores = jnp.where(key_at <= token, scores, -jnp.inf)
@@ -444,109 +547,201 @@
             chances, pair, (((1,), (1,)), ((), ())), preferred_element_type=F32
         )
         for h in range(heads_here):
-            on = me * heads_here + h < active
-            block = mixed[h * length : (h + 1) * length]
-            context[:, h * HD : (h + 1) * HD] = jnp.where(on, block, 0.0).astype(BF16)
-
-    def feed_forward(block_count):
-        def step(i, _):
+            on = me * heads_here + h < heads_on[m, 0]
+            rows = mixed[h * length : (h + 1) * length]
+            context[:, h * HD : (h + 1) * HD] = jnp.where(on, rows, 0.0).astype(BF16)
+        when_loaded(m, 3, 4)
+        scatter(slot, context, v_out, x_in[m, me].astype(F32))
+
+    def scatter(slot, left, weight, base):
+        def to_mate(k, _):
+            at = columns(nth(far, k) * 2 + 1 - core)
+            pair_send[slot, k] = jnp.dot(left[...], weight[:, at], preferred_element_type=F32).astype(BF16)
+            pair_copy(slot, k).start()
+            return 0
+
+        lax.fori_loop(0, chips, to_mate, 0)
+
+        def to_chip(k, _):
+            target = nth(far, k)
+            term = jnp.dot(left[...], weight[:, columns(target * 2 + core)], preferred_element_type=F32)
+            pair_copy(slot, k).wait_recv()
+            i = offset(chip, target)
+            chip_send[slot, i] = (term + pair_in[slot, k].astype(F32)).astype(BF16)
+            chip_copy(slot, target).start()
+            return 0
+
+        lax.fori_loop(0, chips - 1, to_chip, 0)
+        term = jnp.dot(left[...], weight[:, columns(me)], preferred_element_type=F32)
+        residual[slot] = base + term
+
+    def gathered_sum(slot):
+        for k in range(chips):
+            pair_copy(slot, k).wait_send()
+        pair_copy(slot, chips - 1).wait_recv()
+        total = residual[slot] + pair_in[slot, chips - 1].astype(F32)
+        for k in range(chips - 1):
+            pltpu.make_async_copy(chip_in.at[slot, k], chip_in.at[slot, k], chip_recv_sem.at[slot, k]).wait()
+            total = total + chip_in[slot, k].astype(F32)
+            pltpu.make_async_copy(chip_send.at[slot, k], chip_send.at[slot, k], chip_send_sem.at[slot, k]).wait()
+        return total
+
+    def share(m):
+        slot = m % 2
+        attended = gathered_sum(slot)
+        residual[slot] = attended
+        x_ffn[slot, me] = attended.astype(BF16)
+        for o in near[1:]:
+            ffn_direct(slot, o).start()
+        ffn_mate(slot).start()
+
+    def feed_forward(m):
+        slot = m % 2
+        when_loaded(m, 4, 6)
+        squares[...] = jnp.zeros_like(squares)
+
+        def piece(j, first):
+            left = with_gain(1, j, x_ffn[slot, j])
+            rows = columns(j)
+            for weight, acc in ((v_gate, acc_gate), (v_up, acc_up)):
+                term = jnp.dot(left, weight[rows, :], preferred_element_type=F32)
+                acc[...] = term if first else acc[...] + term
+
+        piece(me, True)
+        ffn_mate(slot).wait_recv()
+        piece(mate_at, False)
+
+        def from_chip(i, _):
+            o = nth(near, i)
+            ffn_arrival(slot, o).wait_recv()
+            ffn_relay(slot, o, core).start()
+            piece(o * 2 + core, False)
+            ffn_relay(slot, o, 1 - core).wait_recv()
+            piece(o * 2 + 1 - core, False)
+            return 0
+
+        lax.fori_loop(1, chips, from_chip, 0)
+        scale = row_scale()
+        active = BLOCK * ffn_blocks[m, 0]
+
+        def activate(i, _):
             at = pl.ds(pl.multiple_of(i * TILE, TILE), TILE)
-            left = normed[...]
-            gate = jnp.dot(left, v_gate[:, at], preferred_element_type=F32)
-            up = jnp.dot(left, v_up[:, at], preferred_element_type=F32)
+            gate = acc_gate[:, at] * scale
+            up = acc_up[:, at] * scale
             unit = me * units + i * TILE + lax.broadcasted_iota(jnp.int32, gate.shape, 1)
             value = gate / (1.0 + jnp.exp(-gate)) * up
-            hidden[:, at] = jnp.where(unit < BLOCK * block_count, value, 0.0).astype(BF16)
+            hidden[:, at] = jnp.where(unit < active, value, 0.0).astype(BF16)
             return 0
 
-        lax.fori_loop(0, units // TILE, step, 0)
-
-    def micro_step(m, _):
-        arrived = remote(home, inbox.at[m], outbox_sem.at[0], inbox_sem.at[m], (0, me))
-
-        @pl.when((sec != 0) | (m != 0))
-        def _():
-            arrived.wait_recv()
-
-        rows_f32[...] = inbox[m].astype(F32)
-        norm_rows(attn_gain)
-        all_gather()
-        widen()
-
-        def when_loaded(first, stop):
-            @pl.when(m == 0)
-            def _():
-                for copy in weight_copies()[first:stop]:
-                    copy.wait()
-
-        when_loaded(0, 3)
-        attention(heads_on[m, 0])
-        when_loaded(3, 4)
-        project_rows(context, v_out)
-        reduce_rows()
-        norm_rows(ffn_gain)
-        all_gather()
-        widen()
-        when_loaded(4, 6)
-        feed_forward(ffn_blocks[m, 0])
-        when_loaded(6, 7)
-        project_rows(hidden, v_down)
-        reduce_rows()
-        outbox[m] = rows_f32[...].astype(BF16)
-
-        @pl.when(sec < last)
-        def _():
-            remote(outbox.at[m], inbox.at[m], outbox_sem.at[m], inbox_sem.at[m], (sec + 1, me)).start()
-
-        @pl.when((sec == last) & (m < last))
-        def _():
-            remote(outbox.at[m], home, outbox_sem.at[m], home_sem, (m, me)).start()
-
-        return 0
-
-    lax.fori_loop(0, sections, micro_step, 0)
-
-    for m in range(sections):
-        sent = remote(outbox.at[m], home, outbox_sem.at[m], home_sem, (0, me))
-        if m < last:
-            sent.wait_send()
-        else:
+        lax.fori_loop(0, units // TILE, activate, 0)
+        when_loaded(m, 6, 7)
+        scatter(slot, hidden, v_down, residual[slot])
+        ffn_mate(slot).wait_send()
+        for o in near[1:]:
+            ffn_direct(slot, o).wait_send()
+            ffn_relay(slot, o, core).wait_send()
+
+    def hand_over(m):
+        result[m] = gathered_sum(m % 2).astype(BF16)
+        for o in near:
+            here = (sec == last) & (m == last) & (o == chip)
 
             @pl.when(sec < last)
             def _():
-                sent.wait_send()
-
-    @pl.when(sec < last)
-    def _():
-        remote(outbox.at[0], home, outbox_sem.at[0], home_sem, (last, me)).wait_recv()
-        gathered[slot] = home[...]
-
-    @pl.when(sec == last)
-    def _():
-        gathered[slot] = outbox[last]
-
-    all_gather()
-    done = pltpu.make_async_copy(gathered, out, out_sem)
-    done.start()
-    done.wait()
+                remote(
+                    result.at[m], x_in.at[m, me], result_send.at[m, o], x_recv.at[m, chip], (sec + 1, o * 2 + core)
+                ).start()
+
+            if o is not chip:
+
+                @pl.when(sec == last)
+                def _():
+                    remote(
+                        result.at[m], final.at[me], result_send.at[m, o], final_recv.at[chip], (m, o * 2 + core)
+                    ).start()
+
+        @pl.when((sec == last) & (m != last))
+        def _():
+            remote(
+                result.at[m], final.at[me], result_send.at[m, chip], final_recv.at[chip], (m, me)
+            ).start()
+
+        @pl.when((sec == last) & (m == last))
+        def _():
+            pltpu.make_async_copy(result.at[m], final.at[me], final_recv.at[chip]).start()
+
+    def when_loaded(m, first, stop):
+        @pl.when(m == 0)
+        def _():
+            for copy in weight_copies()[first:stop]:
+                copy.wait()
+
+    def micro_step(m, _):
+        project(m)
+        attend(m)
+
+        @pl.when(m > 0)
+        def _():
+            hand_over(m - 1)
+
+        share(m)
+        feed_forward(m)
+        return 0
+
+    lax.fori_loop(0, sections, micro_step, 0)
+    hand_over(last)
+
+    def drain(m, _):
+        for o in range(chips):
+
+            @pl.when((sec < last) | (m < last) | (o != chip))
+            def _():
+                remote(result.at[m], final.at[me], result_send.at[m, o], final_recv.at[chip], mate).wait_send()
+
+            @pl.when(sec != 0)
+            def _():
+                x_relay(m, o).wait_send()
+
+        return 0
+
+    lax.fori_loop(0, sections, drain, 0)
+
+    def final_copy(o, by):
+        j = o * 2 + by
+        return remote(final.at[j], final.at[j], final_relay_send.at[o], final_relay_recv.at[o], mate)
+
+    def to_output(j):
+        return pltpu.make_async_copy(final.at[j], out.at[:, columns(j)], out_sem.at[j])
+
+    for o in near:
+        j = o * 2 + core
+        remote(final.at[j], final.at[j], result_send.at[0, o], final_recv.at[o], mate).wait_recv()
+        final_copy(o, core).start()
+        to_output(j).start()
+    for o in near:
+        final_copy(o, 1 - core).wait_recv()
+        to_output(o * 2 + 1 - core).start()
+    for o in near:
+        final_copy(o, core).wait_send()
+    for j in range(peers):
+        to_output(j).wait()
 
 
 def resident(hidden_in, attn_gain, w_query, w_key, w_value, w_out, ffn_gain, w_gate, w_up, w_down, ffn_blocks, heads_on):
     sections, peers = lax.axis_size("section"), lax.axis_size("mp")
     length, width = hidden_in.shape[2:]
-    rows, chips = length // peers, peers // 2
+    block, chips = width // peers, peers // 2
     units, key_width = w_gate.shape[2], w_key.shape[2]
     query_width = w_query.shape[2]
     parts_here = key_width // KV_HEADS
-    smem = pl.BlockSpec(memory_space=pltpu.SMEM)
     vmem = pl.BlockSpec(memory_space=pltpu.VMEM)
     hbm = pl.BlockSpec(memory_space=pl.ANY)
     dma = pltpu.SemaphoreType.DMA
     half = pltpu.VMEM
     result = pl.pallas_call(
         lambda *refs: layer_kernel(sections, peers, *refs),
-        out_shape=jax.ShapeDtypeStruct((peers, rows, width), BF16),
-        in_specs=[smem, smem, hbm] + [vmem] * 6 + [hbm] * 7,
+        out_shape=jax.ShapeDtypeStruct((length, width), BF16),
+        in_specs=[hbm] * 3 + [vmem] * 6 + [hbm] * 7,
         out_specs=hbm,
         scratch_shapes=[
             half((width, query_width), BF16),
@@ -555,35 +750,52 @@
             half((width, units), BF16),
             half((width, units), BF16),
             half((units, width), BF16),
-            half((sections, rows, width), BF16),
-            half((sections, rows, width), BF16),
-            half((rows, width), BF16),
-            half((rows, width), F32),
-            half((peers, rows, width), BF16),
+            pltpu.SMEM(heads_on.shape, jnp.int32),
+            pltpu.SMEM(ffn_blocks.shape, jnp.int32),
+            half((2, peers, 8, block), F32),
+            half((sections, peers, length, block), BF16),
+            half((2, peers, length, block), BF16),
+            half((peers, length, block), BF16),
             half((length, width), BF16),
-            half((peers, parts_here, 2 * length), BF16),
-            half((peers, parts_here, 2 * length), BF16),
+            half((length, HD), F32),
+            half((2, length, block), F32),
+            half((2, query_width // HD * length, HD), BF16),
+            half((2, peers, parts_here, 2 * length), BF16),
+            half((2, peers, parts_here, 2 * length), BF16),
             half((length, query_width), BF16),
+            half((length, units), F32),
+            half((length, units), F32),
             half((length, units), BF16),
-            half((peers, rows, width), BF16),
-            half((chips, rows, width), BF16),
-            half((chips - 1, rows, width), BF16),
-            half((chips - 1, rows, width), BF16),
+            half((2, chips, length, block), BF16),
+            half((2, chips, length, block), BF16),
+            half((2, chips - 1, length, block), BF16),
+            half((2, chips - 1, length, block), BF16),
+            half((sections, length, block), BF16),
             dma((7,)),
+            dma((2,)),
+            dma((peers,)),
+            dma,
             dma((sections,)),
-            dma((sections,)),
-            dma,
-            dma,
+            dma((sections, chips)),
+            dma((sections, chips)),
+            dma((sections, chips)),
+            dma((2, peers - 1)),
+            dma((2, peers - 1)),
+            dma((2, chips)),
+            dma((2, chips)),
+            dma((2, chips - 1)),
+            dma((2, chips - 1)),
+            dma((2,)),
+            dma((2,)),
+            dma((2, chips - 1)),
+            dma((2, chips - 1)),
+            dma((2, chips - 1)),
+            dma((2, chips - 1)),
+            dma((sections, chips)),
             dma((chips,)),
             dma((chips,)),
-            dma((chips - 1,)),
-            dma((chips - 1,)),
-            dma((peers - 1,)),
-            dma((peers - 1,)),
-            dma((2,)),
-            dma((chips - 1,)),
-            dma((chips - 1,)),
-            dma,
+            dma((chips,)),
+            dma((peers,)),
         ],
         compiler_params=pltpu.CompilerParams(
             collective_id=0, has_side_effects=True, vmem_limit_bytes=67043328
@@ -591,7 +803,7 @@
     )(
         heads_on,
         ffn_blocks,
-        hidden_in.reshape(peers, rows, width),
+        hidden_in.reshape(length, width),
         attn_gain,
         ffn_gain,
         *tables(length),
@@ -613,12 +825,14 @@
         hidden_in.shape[0] == 1
         and args[10].shape[0] == sections
         and peers == KV_HEADS
-        and hidden_in.shape[2] == 8 * peers
+        and sections == 4
+        and args[5].shape[1] == w_query.shape[2]
         and 2 * hidden_in.shape[2] == HD
         and w_query.shape[2] * KV_HEADS == HEADS * HD
         and w_key.shape[2] == HD
         and w_gate.shape[2] % TILE == 0
-        and hidden_in.shape[3] % WIDE == 0
+        and hidden_in.shape[3] % (peers * HD) == 0
+        and hidden_in.shape[3] == HEADS * HD
     )
     return (resident if fits else per_device)(*args)
 

time: 391 us -> 338 us (0.86)
  Pallas kernels: 386 us -> 334 us
    pallas_call x1, Pallas kernels: 386 us -> 334 us  [resident(): pl.pallas_call(lambda *refs: layer_kernel(sections, peers, *refs), out_sh...]
where the time goes in v1:
time: 338 us
  Pallas kernels  334 us (99%)
  local copies, waits for them, and re-layouts  4.51 us (1%)
    pallas_call x1, Pallas kernels, resident(): pl.pallas_call(lambda *refs: layer_kernel(sections, peers, *refs), out_sh...  334 us

profile of v1, /device:TPU:7, one launch (start us, length us, event | category | flops | bytes accessed | tf_op | source)
XLA Modules:
  0.0 338.1 jit_solution(17085051534524629633)
XLA Ops:
  0.0 1.3 copy.18.refs_1_
  1.3 1.3 copy.17.refs_0_
  2.6 333.5 %shard_map.154 = bf16[64,4096]{1,0:T(8,128)(2,1)} custom-call(s32[4,1]{1,0:T(4,128)} %copy.17.refs_0_, s32[4,1]{1,0:T(4,128)} %copy.18.refs_1_, bf16[64,4096]{1,0:T(8,128)(2,1)} %bitcast.17, bf16[1,4096]{1,0:T(2,128)(2,1)} %refs_3_.1, bf16[1,4096]{1,0:T(2,128)(2,1)} %refs_4_.1, f32[64,128]{1,0:T(8,128)} %constant.8.clone.refs_5_, ...), custom_call_target="tpu_custom_call" | custom-call | tf_op jit(solution)/shard_map/pallas_call | solution.py:741
  336.2 1.9 copy.20

commit v2 on v1

--- a/solution.py
+++ b/solution.py
@@ -252,6 +252,9 @@
     squares,
     residual,
     query_buf,
+    key_buf,
+    value_buf,
+    mixed_buf,
     kv_send,
     kv_recv,
     context,
@@ -264,6 +267,8 @@
     chip_in,
     result,
     weight_sem,
+    head_send_sem,
+    head_recv_sem,
     small_sem,
     stage_sem,
     seed_send,
@@ -354,8 +359,13 @@
         for copy in staged(final):
             copy.start()
 
-    for copy in weight_copies():
+    for copy in weight_copies()[:2]:
         copy.start()
+
+    @pl.when(sec == 0)
+    def _():
+        for copy in weight_copies()[2:]:
+            copy.start()
 
     barrier = pltpu.get_barrier_semaphore()
     for step in range(1, peers):
@@ -391,9 +401,80 @@
     for copy in small:
         copy.wait()
 
+    parts_here = key_width // KV_HEADS
+    tile_row = lax.broadcasted_iota(jnp.int32, (key_width, key_width), 0)
+    tile_col = lax.broadcasted_iota(jnp.int32, (key_width, key_width), 1)
+    by_heads = tile_col == tile_row % parts_here * KV_HEADS + tile_row // parts_here
+    pick = jnp.where(by_heads, 1.0, 0.0).astype(BF16)
+    same = jnp.where(tile_col == tile_row, 1.0, 0.0).astype(BF16)
+
+    def head_rows(which, by, received):
+        at = received * 2 * key_width + which * key_width + by * parts_here
+        return v_down.at[pl.ds(pl.multiple_of(at, parts_here), parts_here), :]
+
+    def head_copy(which, k, b):
+        to = far[k] * 2 + (1 - core if b else core)
+        i = offset(chip, far[k]) * 2 + b if k < chips - 1 else peers - 2
+        return remote(
+            head_rows(which, to, 0),
+            head_rows(which, me, 1),
+            head_send_sem.at[which, i],
+            head_recv_sem.at[which, i],
+            (sec, to),
+        )
+
+    def head_arrival(which, k, b):
+        by = far[k] * 2 + (1 - core if b else core)
+        i = offset(far[k], chip) * 2 + b if k < chips - 1 else peers - 2
+        there = head_rows(which, by, 1)
+        return remote(there, there, head_send_sem.at[which, i], head_recv_sem.at[which, i], mate)
+
+    head_order = [(k, b) for k in range(chips - 1) for b in range(2)] + [(chips - 1, 1)]
+
+    def stripe(i):
+        return pl.ds(pl.multiple_of(i * block, block), block)
+
     @pl.when(sec != 0)
     def _():
         seed.wait_send()
+        for copy in weight_copies()[:2]:
+            copy.wait()
+
+        for which in range(2):
+            rows = pl.ds(which * key_width, key_width)
+
+            def to_heads(i, _):
+                turned = lax.dot_general(
+                    pick, v_kv[stripe(i), rows], (((1,), (1,)), ((), ())), preferred_element_type=F32
+                )
+                v_down[rows, stripe(i)] = turned.astype(BF16)
+                return 0
+
+            lax.fori_loop(0, peers, to_heads, 0)
+            for k, b in head_order:
+                head_copy(which, k, b).start()
+            own = pl.multiple_of(which * key_width + me * parts_here, parts_here)
+            v_down[pl.ds(2 * key_width + own, parts_here), :] = v_down[pl.ds(own, parts_here), :]
+        for copy in weight_copies()[2:-1]:
+            copy.start()
+        for which in range(2):
+            for k, b in head_order:
+                head_copy(which, k, b).wait_send()
+                head_arrival(which, k, b).wait_recv()
+            rows = pl.ds(which * key_width, key_width)
+
+            def from_heads(i, _):
+                turned = lax.dot_general(
+                    v_down[pl.ds((2 + which) * key_width, key_width), stripe(i)],
+                    same,
+                    (((0,), (0,)), ((), ())),
+                    preferred_element_type=F32,
+                )
+                v_kv[stripe(i), rows] = turned.astype(BF16)
+                return 0
+
+            lax.fori_loop(0, peers, from_heads, 0)
+        weight_copies()[-1].start()
 
     def row_scale():
         total = jnp.sum(squares[...], axis=-1, keepdims=True)
@@ -506,22 +587,33 @@
             return 0
 
         lax.fori_loop(0, chips, relayed, 0)
-        when_loaded(m, 0, 3)
+
+        @pl.when(sec == 0)
+        def _():
+            when_loaded(m, 0, 2)
+
+        when_loaded(m, 2, 3)
         scale = row_scale()
         left = scaled[...]
         kv = (jnp.dot(left, v_kv[...], preferred_element_type=F32) * scale).astype(BF16)
-        stacked = jnp.concatenate([kv[:, :key_width], kv[:, key_width:]], axis=0)
-        r = lax.broadcasted_iota(jnp.int32, (key_width, key_width), 0)
-        c = lax.broadcasted_iota(jnp.int32, (key_width, key_width), 1)
-        parts_here = key_width // KV_HEADS
-        pick = jnp.where(c == (r % parts_here) * KV_HEADS + r // parts_here, 1.0, 0.0).astype(BF16)
-        by_head = lax.dot_general(
-            pick, stacked, (((1,), (1,)), ((), ())), preferred_element_type=F32
-        )
-        kv_send[slot] = by_head.astype(BF16).reshape(KV_HEADS, parts_here, 2 * length)
-        for step in range(1, peers):
-            kv_copy(slot, step).start()
-        kv_recv[slot, me] = kv_send[slot, me]
+
+        @pl.when(sec == 0)
+        def _():
+            stacked = jnp.concatenate([kv[:, :key_width], kv[:, key_width:]], axis=0)
+            by_head = lax.dot_general(
+                pick, stacked, (((1,), (1,)), ((), ())), preferred_element_type=F32
+            )
+            kv_send[slot] = by_head.astype(BF16).reshape(KV_HEADS, parts_here, 2 * length)
+            for step in range(1, peers):
+                kv_copy(slot, step).start()
+            kv_recv[slot, me] = kv_send[slot, me]
+
+        @pl.when(sec != 0)
+        def _():
+            key = kv[:, :key_width].astype(F32)
+            key_buf[...] = (key * q_cos[...] + pltpu.roll(key, HD // 2, 1) * q_sin[...]).astype(BF16)
+            value_buf[...] = kv[:, key_width:]
+
         query = jnp.dot(left, v_query[...], preferred_element_type=F32) * scale
         for h in range(heads_here):
             head = query[:, h * HD : (h + 1) * HD]
@@ -531,23 +623,37 @@
 
     def attend(m):
         slot = m % 2
-        for step in range(1, peers):
-            kv_copy(slot, step).wait()
-        pair = kv_recv[slot].reshape(HD, 2 * length).astype(F32)
-        swapped = jnp.concatenate([pair[HD // 2 :], pair[: HD // 2]], axis=0)
-        pair = (pair * k_cos[...] + swapped * k_sin[...]).astype(BF16)
-        scores = jnp.dot(query_buf[slot], pair, preferred_element_type=F32) * HD ** (-0.5)
-        token = lax.broadcasted_iota(jnp.int32, scores.shape, 0) % length
-        key_at = lax.broadcasted_iota(jnp.int32, scores.shape, 1)
-        scores = jnp.where(key_at <= token, scores, -jnp.inf)
-        scores = jnp.exp(scores - jnp.max(scores, axis=-1, keepdims=True))
-        chances = scores / jnp.sum(scores, axis=-1, keepdims=True)
-        chances = pltpu.roll(chances, length, 1).astype(BF16)
-        mixed = lax.dot_general(
-            chances, pair, (((1,), (1,)), ((), ())), preferred_element_type=F32
-        )
+
+        def mix(key, value, value_side, shift):
+            sides = (((1,), (1 - value_side,)), ((), ()))
+            scores = lax.dot_general(query_buf[slot], key, sides, preferred_element_type=F32) * HD ** (-0.5)
+            token = lax.broadcasted_iota(jnp.int32, scores.shape, 0) % length
+            key_at = lax.broadcasted_iota(jnp.int32, scores.shape, 1)
+            scores = jnp.where(key_at <= token, scores, -jnp.inf)
+            scores = jnp.exp(scores - jnp.max(scores, axis=-1, keepdims=True))
+            chances = scores / jnp.sum(scores, axis=-1, keepdims=True)
+            if shift:
+                chances = pltpu.roll(chances, length, 1)
+            mixed_buf[...] = lax.dot_general(
+                chances.astype(BF16), value, (((1,), (value_side,)), ((), ())), preferred_element_type=F32
+            )
+
+        @pl.when(sec == 0)
+        def _():
+            for step in range(1, peers):
+                kv_copy(slot, step).wait()
+            pair = kv_recv[slot].reshape(HD, 2 * length).astype(F32)
+            swapped = jnp.concatenate([pair[HD // 2 :], pair[: HD // 2]], axis=0)
+            pair = (pair * k_cos[...] + swapped * k_sin[...]).astype(BF16)
+            mix(pair, pair, 1, True)
+
+        @pl.when(sec != 0)
+        def _():
+            mix(key_buf[...], value_buf[...], 0, False)
+
+        mixed = mixed_buf[...]
         for h in range(heads_here):
-            on = me * heads_here + h < heads_on[m, 0]
+            on = me * heads_here + h < heads_on[0, m]
             rows = mixed[h * length : (h + 1) * length]
             context[:, h * HD : (h + 1) * HD] = jnp.where(on, rows, 0.0).astype(BF16)
         when_loaded(m, 3, 4)
@@ -622,7 +728,7 @@
 
         lax.fori_loop(1, chips, from_chip, 0)
         scale = row_scale()
-        active = BLOCK * ffn_blocks[m, 0]
+        active = BLOCK * ffn_blocks[0, m]
 
         def activate(i, _):
             at = pl.ds(pl.multiple_of(i * TILE, TILE), TILE)
@@ -677,19 +783,22 @@
                 copy.wait()
 
     def micro_step(m, _):
-        project(m)
+        @pl.when((sec != 0) | (m == 0))
+        def _():
+            project(m)
+
         attend(m)
 
-        @pl.when(m > 0)
-        def _():
-            hand_over(m - 1)
+        @pl.when((sec == 0) & (m < last))
+        def _():
+            project(m + 1)
 
         share(m)
         feed_forward(m)
+        hand_over(m)
         return 0
 
     lax.fori_loop(0, sections, micro_step, 0)
-    hand_over(last)
 
     def drain(m, _):
         for o in range(chips):
@@ -750,8 +859,8 @@
             half((width, units), BF16),
             half((width, units), BF16),
             half((units, width), BF16),
-            pltpu.SMEM(heads_on.shape, jnp.int32),
-            pltpu.SMEM(ffn_blocks.shape, jnp.int32),
+            pltpu.SMEM((1, sections), jnp.int32),
+            pltpu.SMEM((1, sections), jnp.int32),
             half((2, peers, 8, block), F32),
             half((sections, peers, length, block), BF16),
             half((2, peers, length, block), BF16),
@@ -760,6 +869,9 @@
             half((length, HD), F32),
             half((2, length, block), F32),
             half((2, query_width // HD * length, HD), BF16),
+            half((length, HD), BF16),
+            half((length, HD), BF16),
+            half((query_width // HD * length, HD), F32),
             half((2, peers, parts_here, 2 * length), BF16),
             half((2, peers, parts_here, 2 * length), BF16),
             half((length, query_width), BF16),
@@ -772,6 +884,8 @@
             half((2, chips - 1, length, block), BF16),
             half((sections, length, block), BF16),
             dma((7,)),
+            dma((2, peers - 1)),
+            dma((2, peers - 1)),
             dma((2,)),
             dma((peers,)),
             dma,
@@ -801,8 +915,8 @@
             collective_id=0, has_side_effects=True, vmem_limit_bytes=67043328
         ),
     )(
-        heads_on,
-        ffn_blocks,
+        heads_on.T,
+        ffn_blocks.T,
         hidden_in.reshape(length, width),
         attn_gain,
         ffn_gain,

time: 338 us -> 288 us (0.85)
  Pallas kernels: 334 us -> 285 us
    pallas_call x1, Pallas kernels: 334 us -> 285 us  [resident(): pl.pallas_call(lambda *refs: layer_kernel(sections, peers, *refs), out_sh...]
where the time goes in v2:
time: 288 us; the launch traced here: 287 us
  Pallas kernels  285 us (99%)
    pallas_call x1, Pallas kernels, resident(): pl.pallas_call(lambda *refs: layer_kernel(sections, peers, *refs), out_sh...  285 us

profile of v2, /device:TPU:7, one launch (start us, length us, event | category | flops | bytes accessed | tf_op | source)
XLA Modules:
  0.0 287.4 jit_solution(5680655551282584168)
XLA Ops:
  0.0 285.5 %shard_map.154 = bf16[64,4096]{1,0:T(8,128)(2,1)} custom-call(s32[1,4]{1,0:T(1,128)} %bitcast.20, s32[1,4]{1,0:T(1,128)} %bitcast.21, bf16[64,4096]{1,0:T(8,128)(2,1)} %bitcast.19, bf16[1,4096]{1,0:T(2,128)(2,1)} %refs_3_.1, bf16[1,4096]{1,0:T(2,128)(2,1)} %refs_4_.1, f32[64,128]{1,0:T(8,128)} %constant.8.clone.refs_5_, f32[64,128]{1,0:T(8,128)} %constant.9.clone.refs_6_, ...), custom_call_target="tpu_custom_call" | custom-call | tf_op jit(solution)/shard_map/pallas_call | solution.py:850
  285.5 1.9 copy.18

commit v3 on v2

--- a/solution.py
+++ b/solution.py
@@ -511,18 +511,18 @@
             (sec, to),
         )
 
-    def pair_copy(slot, k):
+    def pair_copy(m, k):
         return remote(
-            pair_send.at[slot, k], pair_in.at[slot, k], pair_send_sem.at[slot, k], pair_recv_sem.at[slot, k], mate
-        )
-
-    def chip_copy(slot, target):
+            pair_send.at[m % 2, k], pair_in.at[m, k], pair_send_sem.at[m, k], pair_recv_sem.at[m, k], mate
+        )
+
+    def chip_copy(m, target):
         i = offset(chip, target)
         return remote(
-            chip_send.at[slot, i],
-            chip_in.at[slot, i],
-            chip_send_sem.at[slot, i],
-            chip_recv_sem.at[slot, i],
+            chip_send.at[m % 2, i],
+            chip_in.at[m, i],
+            chip_send_sem.at[m, i],
+            chip_recv_sem.at[m, i],
             (sec, target * 2 + core),
         )
 
@@ -657,13 +657,13 @@
             rows = mixed[h * length : (h + 1) * length]
             context[:, h * HD : (h + 1) * HD] = jnp.where(on, rows, 0.0).astype(BF16)
         when_loaded(m, 3, 4)
-        scatter(slot, context, v_out, x_in[m, me].astype(F32))
-
-    def scatter(slot, left, weight, base):
+        scatter(m, context, v_out, x_in[m, me].astype(F32))
+
+    def scatter(m, left, weight, base):
         def to_mate(k, _):
             at = columns(nth(far, k) * 2 + 1 - core)
-            pair_send[slot, k] = jnp.dot(left[...], weight[:, at], preferred_element_type=F32).astype(BF16)
-            pair_copy(slot, k).start()
+            pair_send[m % 2, k] = jnp.dot(left[...], weight[:, at], preferred_element_type=F32).astype(BF16)
+            pair_copy(m, k).start()
             return 0
 
         lax.fori_loop(0, chips, to_mate, 0)
@@ -671,30 +671,30 @@
         def to_chip(k, _):
             target = nth(far, k)
             term = jnp.dot(left[...], weight[:, columns(target * 2 + core)], preferred_element_type=F32)
-            pair_copy(slot, k).wait_recv()
+            pair_copy(m, k).wait_recv()
             i = offset(chip, target)
-            chip_send[slot, i] = (term + pair_in[slot, k].astype(F32)).astype(BF16)
-            chip_copy(slot, target).start()
+            chip_send[m % 2, i] = (term + pair_in[m, k].astype(F32)).astype(BF16)
+            chip_copy(m, target).start()
             return 0
 
         lax.fori_loop(0, chips - 1, to_chip, 0)
         term = jnp.dot(left[...], weight[:, columns(me)], preferred_element_type=F32)
-        residual[slot] = base + term
-
-    def gathered_sum(slot):
+        residual[m % 2] = base + term
+
+    def gathered_sum(m):
         for k in range(chips):
-            pair_copy(slot, k).wait_send()
-        pair_copy(slot, chips - 1).wait_recv()
-        total = residual[slot] + pair_in[slot, chips - 1].astype(F32)
+            pair_copy(m, k).wait_send()
+        pair_copy(m, chips - 1).wait_recv()
+        total = residual[m % 2] + pair_in[m, chips - 1].astype(F32)
         for k in range(chips - 1):
-            pltpu.make_async_copy(chip_in.at[slot, k], chip_in.at[slot, k], chip_recv_sem.at[slot, k]).wait()
-            total = total + chip_in[slot, k].astype(F32)
-            pltpu.make_async_copy(chip_send.at[slot, k], chip_send.at[slot, k], chip_send_sem.at[slot, k]).wait()
+            pltpu.make_async_copy(chip_in.at[m, k], chip_in.at[m, k], chip_recv_sem.at[m, k]).wait()
+            total = total + chip_in[m, k].astype(F32)
+            pltpu.make_async_copy(chip_send.at[m % 2, k], chip_send.at[m % 2, k], chip_send_sem.at[m, k]).wait()
         return total
 
     def share(m):
         slot = m % 2
-        attended = gathered_sum(slot)
+        attended = gathered_sum(m)
         residual[slot] = attended
         x_ffn[slot, me] = attended.astype(BF16)
         for o in near[1:]:
@@ -726,7 +726,13 @@
             piece(o * 2 + 1 - core, False)
             return 0
 
-        lax.fori_loop(1, chips, from_chip, 0)
+        lax.fori_loop(1, 3, from_chip, 0)
+
+        @pl.when(m % 2 == 0)
+        def _():
+            share(m + 1)
+
+        lax.fori_loop(3, chips, from_chip, 0)
         scale = row_scale()
         active = BLOCK * ffn_blocks[0, m]
 
@@ -741,14 +747,19 @@
 
         lax.fori_loop(0, units // TILE, activate, 0)
         when_loaded(m, 6, 7)
-        scatter(slot, hidden, v_down, residual[slot])
+
+        @pl.when(m % 2 == 1)
+        def _():
+            hand_over(m - 1)
+
+        scatter(m, hidden, v_down, residual[slot])
         ffn_mate(slot).wait_send()
         for o in near[1:]:
             ffn_direct(slot, o).wait_send()
             ffn_relay(slot, o, core).wait_send()
 
     def hand_over(m):
-        result[m] = gathered_sum(m % 2).astype(BF16)
+        result[m] = gathered_sum(m).astype(BF16)
         for o in near:
             here = (sec == last) & (m == last) & (o == chip)
 
@@ -782,23 +793,34 @@
             for copy in weight_copies()[first:stop]:
                 copy.wait()
 
-    def micro_step(m, _):
-        @pl.when((sec != 0) | (m == 0))
-        def _():
-            project(m)
-
-        attend(m)
-
-        @pl.when((sec == 0) & (m < last))
-        def _():
-            project(m + 1)
-
-        share(m)
-        feed_forward(m)
-        hand_over(m)
+    def both(g, _):
+        def first_half(i, _):
+            @pl.when(i < 2)
+            def _():
+                project(2 * g + i)
+
+            now = jnp.where(sec == 0, i - 1, i)
+
+            @pl.when((now >= 0) & (now < 2))
+            def _():
+                attend(2 * g + now)
+
+            @pl.when(now == 0)
+            def _():
+                share(2 * g)
+
+            return 0
+
+        def second_half(i, _):
+            feed_forward(2 * g + i)
+            return 0
+
+        lax.fori_loop(0, 3, first_half, 0)
+        lax.fori_loop(0, 2, second_half, 0)
+        hand_over(2 * g + 1)
         return 0
 
-    lax.fori_loop(0, sections, micro_step, 0)
+    lax.fori_loop(0, sections // 2, both, 0)
 
     def drain(m, _):
         for o in range(chips):
@@ -879,9 +901,9 @@
             half((length, units), F32),
             half((length, units), BF16),
             half((2, chips, length, block), BF16),
-            half((2, chips, length, block), BF16),
+            half((sections, chips, length, block), BF16),
             half((2, chips - 1, length, block), BF16),
-            half((2, chips - 1, length, block), BF16),
+            half((sections, chips - 1, length, block), BF16),
             half((sections, length, block), BF16),
             dma((7,)),
             dma((2, peers - 1)),
@@ -895,10 +917,10 @@
             dma((sections, chips)),
             dma((2, peers - 1)),
             dma((2, peers - 1)),
-            dma((2, chips)),
-            dma((2, chips)),
-            dma((2, chips - 1)),
-            dma((2, chips - 1)),
+            dma((sections, chips)),
+            dma((sections, chips)),
+            dma((sections, chips - 1)),
+            dma((sections, chips - 1)),
             dma((2,)),
             dma((2,)),
             dma((2, chips - 1)),

time: 288 us -> 281 us (0.976)
  Pallas kernels: 285 us -> 279 us
    pallas_call x1, Pallas kernels: 285 us -> 279 us  [resident(): pl.pallas_call(lambda *refs: layer_kernel(sections, peers, *refs), out_sh...]
where the time goes in v3:
time: 281 us
  Pallas kernels  279 us (99%)
    pallas_call x1, Pallas kernels, resident(): pl.pallas_call(lambda *refs: layer_kernel(sections, peers, *refs), out_sh...  279 us

profile of v3, /device:TPU:7, one launch (start us, length us, event | category | flops | bytes accessed | tf_op | source)
XLA Modules:
  0.0 281.2 jit_solution(9864946105963110024)
XLA Ops:
  0.0 279.3 %shard_map.154 = bf16[64,4096]{1,0:T(8,128)(2,1)} custom-call(s32[1,4]{1,0:T(1,128)} %bitcast.20, s32[1,4]{1,0:T(1,128)} %bitcast.21, bf16[64,4096]{1,0:T(8,128)(2,1)} %bitcast.19, bf16[1,4096]{1,0:T(2,128)(2,1)} %refs_3_.1, bf16[1,4096]{1,0:T(2,128)(2,1)} %refs_4_.1, f32[64,128]{1,0:T(8,128)} %constant.8.clone.refs_5_, f32[64,128]{1,0:T(8,128)} %constant.9.clone.refs_6_, ...), custom_call_target="tpu_custom_call" | custom-call | tf_op jit(solution)/shard_map/pallas_call | solution.py:872
  279.3 1.9 copy.18
